TPU v7x, 32 devices: a whole 2x2x4 slice. The times are simulated.
32 devices in a mesh: dp: 4 (over x, core), hist: 8 (over z, y).
Axes of the slice: x: 2, y: 2, z: 4, core: 2. Of those that a mesh axis runs over, the one named last changes fastest.
Arguments:
- candidates: bfloat16 [16, 512, 128], P('dp', 'hist'), may hold values from -150 to 150
- history: bfloat16 [16, 16384, 128], P('dp', 'hist'), may hold values from -6 to 6
- projections: bfloat16 [4, 128, 128], P(None, 'dp'), may hold values from -0.5 to 0.5
- lengths: int32 [16], P('dp'), may hold values from 8193 to 16384
- selected: int32 [16, 64], P('dp'), may hold values from 0 to 127, as said below
Outputs:
- interest: bfloat16 [16, 512, 128], P('dp', 'hist')
Inputs may be any that keep to these rules, and one draw needn't show every extreme that they name: `selected`: each row names 64 different history blocks.
All inputs are finite; a program needn't handle non-finite values.
Results may differ from a plain program's by a relative error of at most 0.008.
The roundings to bfloat16 on the way count: a program that leaves them out, or rounds other values in their place, can miss the bound.
Values may be sent and summed in bfloat16 or wider, within the bound.
A program may use at most 128 MiB of HBM per device.

v0:
```python
import math

import jax
import jax.numpy as jnp
from jax import lax
from jax.sharding import PartitionSpec as P

D = 128
H = 4
BLOCK = 128


def scale_heads(blocks, factor):
    layout = blocks.shape
    heads = factor.shape[-1]
    return (blocks.reshape(layout[:-1] + (heads, layout[-1] // heads)) * factor[..., None]).reshape(
        layout
    )


def body(candidates, history, projections, lengths, selected):
    weights = lax.all_gather(projections, "dp", axis=1, tiled=True)
    user_count, own_cands, embed = candidates.shape
    head_size = D // H
    inv_root = 1.0 / math.sqrt(head_size)
    whole = lax.all_gather(candidates, "hist", axis=1, tiled=True)
    queries = jnp.dot(whole.reshape(-1, embed), weights[0], preferred_element_type=jnp.float32)
    queries = queries.astype(jnp.bfloat16).reshape(user_count, -1, embed)
    cand_count = queries.shape[1]
    own_rows = history.shape[1]
    key_value = jnp.concatenate([weights[1], weights[2]], axis=1)
    projected = jnp.dot(history.reshape(-1, embed), key_value, preferred_element_type=jnp.float32)
    projected = projected.astype(jnp.bfloat16).reshape(user_count, own_rows, 2 * embed)
    keys = projected[:, :, :embed]
    values = projected[:, :, embed:]
    places = lax.axis_index("hist") * own_rows + jnp.arange(own_rows, dtype=jnp.int32)
    block_ids = places // BLOCK
    chosen = jnp.any(selected[:, :, None] == block_ids[None, None, :], axis=1)
    live = jnp.logical_and(chosen, places[None, :] < lengths[:, None])
    span = min(512, own_rows)
    pieces = own_rows // span

    def attend(item):
        query_rows, key_rows, value_rows, live_row = item
        query_heads = query_rows.reshape(cand_count, H, head_size)

        def one_piece(sub):
            key_part, value_part, live_part = sub
            scores = (
                jnp.einsum(
                    "chd,khd->hck",
                    query_heads,
                    key_part.reshape(span, H, head_size),
                    preferred_element_type=jnp.float32,
                )
                * inv_root
            )
            scores = jnp.where(live_part[None, None, :], scores, -1e30)
            maxima = jnp.max(scores, axis=-1)
            expo = jnp.where(live_part[None, None, :], jnp.exp(scores - maxima[:, :, None]), 0.0)
            totals = jnp.sum(expo, axis=-1)
            summed = jnp.einsum(
                "hck,khd->chd",
                expo.astype(jnp.bfloat16),
                value_part.reshape(span, H, head_size),
                preferred_element_type=jnp.float32,
            )
            return (maxima.T, totals.T, summed.reshape(cand_count, embed))

        maxima_all, totals_all, summed_all = lax.map(
            one_piece,
            (
                key_rows.reshape(pieces, span, embed),
                value_rows.reshape(pieces, span, embed),
                live_row.reshape(pieces, span),
            ),
        )
        highest = jnp.max(maxima_all, axis=0)
        factors = jnp.exp(maxima_all - highest[None])
        totals = jnp.sum(totals_all * factors, axis=0)
        summed = jnp.sum(scale_heads(summed_all, factors), axis=0)
        return (highest, totals, summed)

    def per_user(item):
        return attend(item)

    maxima, totals, summed = lax.map(per_user, (queries, keys, values, live))
    maxima_all, totals_all, summed_all = (
        lax.all_to_all(maxima[None], "hist", split_axis=2, concat_axis=0, tiled=True),
        lax.all_to_all(totals[None], "hist", split_axis=2, concat_axis=0, tiled=True),
        lax.all_to_all(summed[None], "hist", split_axis=2, concat_axis=0, tiled=True),
    )
    highest = jnp.max(maxima_all, axis=0)
    factors = jnp.exp(maxima_all - highest[None])
    totals = jnp.sum(totals_all * factors, axis=0)
    summed = jnp.sum(scale_heads(summed_all, factors), axis=0)
    attended = scale_heads(summed, 1.0 / totals).astype(jnp.bfloat16)
    interest = jnp.dot(attended.reshape(-1, embed), weights[3], preferred_element_type=jnp.float32)
    return interest.astype(jnp.bfloat16).reshape(user_count, own_cands, embed)


def solution(mesh):
    placed = (
        P("dp", "hist", None),
        P("dp", "hist", None),
        P(None, "dp", None),
        P("dp"),
        P("dp", None),
    )
    return jax.shard_map(
        body, mesh=mesh, in_specs=placed, out_specs=P("dp", "hist", None), check_vma=False
    )
```

profile of v0, /device:TPU:12, one launch (start us, length us, event | category | flops | bytes accessed | tf_op | source)
XLA Modules:
  0.0 319.5 jit_solution(1402405281978077282)
XLA Ops:
  0.0 5.8 %all_gather.6 = bf16[4,128,128]{2,1,0:T(8,128)(2,1)S(1)} all-gather(bf16[4,32,128]{2,1,0:T(8,128)(2,1)} %param.11), channel_id=1, replica_groups=mesh['dp'=4,'hist'=8] {'dp'}, dimensions={1}, use_global_device_ids=true | all-gather | bytes 163840 | tf_op jit(solution)/shard_map/all_gather | solution.py:22
  5.8 3.3 %fusion.12 = bf16[8192,256]{0,1:T(8,128)(2,1)} fusion(bf16[8192,128]{1,0:T(8,128)(2,1)S(1)} %bitcast.121, bf16[128,128]{1,0:T(8,128)(2,1)S(1)} %get-tuple-element.245, bf16[128,128]{1,0:T(8,128)(2,1)S(1)} %get-tuple-element.244), kind=kOutput, calls=%fused_computation.30 | convolution fusion | flops 539099136 | bytes 6356992 | tf_op jit(solution)/shard_map/dot_general | solution.py:32
  9.1 6.4 %copy.83 = bf16[8192,256]{1,0:T(8,128)(2,1)} copy(bf16[8192,256]{0,1:T(8,128)(2,1)} %fusion.12) | data formatting | bytes 8388608 | tf_op jit(solution)/shard_map/reshape | solution.py:33
  15.5 4.5 %fusion.20 = (bf16[4,2048,128]{2,1,0:T(8,128)(2,1)}, bf16[4,2048,128]{2,1,0:T(8,128)(2,1)}) fusion(bf16[4,2048,256]{2,1,0:T(8,128)(2,1)} %bitcast.129), kind=kLoop, calls=%fused_computation.57 | loop fusion | bytes 8388608 | tf_op jit(solution)/shard_map/slice | solution.py:35
  20.0 28.9 %all_gather.7 = bf16[4,512,128]{2,1,0:T(8,128)(2,1)S(1)} all-gather(bf16[4,64,128]{2,1,0:T(8,128)(2,1)S(1)} %copy-done.3), channel_id=1, replica_groups=mesh['dp'=4,'hist'=8] {'hist'}, dimensions={1}, use_global_device_ids=true | all-gather | bytes 589824 | tf_op jit(solution)/shard_map/all_gather | solution.py:26
  51.1 207.6 %while.29 = (s32[]{:T(128)}, f32[4,512,4]{1,2,0:T(4,128)}, f32[4,512,4]{1,2,0:T(4,128)}, f32[4,512,128]{2,0,1:T(4,128)}, bf16[4,2048,128]{2,1,0:T(8,128)(2,1)}, ...) while((s32[]{:T(128)}, f32[4,512,4]{1,2,0:T(4,128)}, ...), condition=%wide.region_9.10_spmd, body=%wide.region_1.9_spmd.sunk | while | flops 148332544 | bytes 36866940 | solution.py:87
  55.0 36.4 %while.30 = (s32[]{:T(128)}, f32[4,512,4]{1,2,0:T(4,128)}, f32[4,512,4]{1,2,0:T(4,128)}, f32[4,512,128]{1,2,0:T(8,128)}, pred[4,512]{1,0:T(4,128)(4,1)S(1)}, /*i...) while((s32[]{:T(128)}, f32[4,512,4]{1,2,0:T(4,128)}, ...), condition=%wide.region_5.5_spmd, body=%wide.region_2.4_spmd.sunk | while | flops 147845120 | bytes 31656596 | solution.py:70
  56.3 1.9 copy-done.1
  60.2 3.2 %fusion.40 = f32[4,32,512]{2,1,0:T(8,128)S(1)} fusion(bf16[512,4,32]{0,2,1:T(8,128)(2,1)S(1)} %bitcast.125, f32[4,512,512]{2,1,0:T(8,128)} %copy-done.1, f32[4,512]{1,0:T(4,128)S(1)} %get-tuple-element.380, pred[512]{0:T(512)(128)(4,1)S(1)} %dynamic-slice_reduce_fusion.5), kind=kOutput, calls=%fused_computation.7.clone.1 | convolution fusion | flops 72351744 | bytes 4596224 | tf_op jit(solution)/shard_map/while/body/eval_jaxpr/while/body/eval_jaxpr/hck,khd->chd/dot_general | solution.py:62
  65.4 1.9 copy-done.1
  69.2 3.2 %fusion.40 = f32[4,32,512]{2,1,0:T(8,128)S(1)} fusion(bf16[512,4,32]{0,2,1:T(8,128)(2,1)S(1)} %bitcast.125, f32[4,512,512]{2,1,0:T(8,128)} %copy-done.1, f32[4,512]{1,0:T(4,128)S(1)} %get-tuple-element.380, pred[512]{0:T(512)(128)(4,1)S(1)} %dynamic-slice_reduce_fusion.5), kind=kOutput, calls=%fused_computation.7.clone.1 | convolution fusion | flops 72351744 | bytes 4596224 | tf_op jit(solution)/shard_map/while/body/eval_jaxpr/while/body/eval_jaxpr/hck,khd->chd/dot_general | solution.py:62
  74.5 1.9 copy-done.1
  78.3 3.2 %fusion.40 = f32[4,32,512]{2,1,0:T(8,128)S(1)} fusion(bf16[512,4,32]{0,2,1:T(8,128)(2,1)S(1)} %bitcast.125, f32[4,512,512]{2,1,0:T(8,128)} %copy-done.1, f32[4,512]{1,0:T(4,128)S(1)} %get-tuple-element.380, pred[512]{0:T(512)(128)(4,1)S(1)} %dynamic-slice_reduce_fusion.5), kind=kOutput, calls=%fused_computation.7.clone.1 | convolution fusion | flops 72351744 | bytes 4596224 | tf_op jit(solution)/shard_map/while/body/eval_jaxpr/while/body/eval_jaxpr/hck,khd->chd/dot_general | solution.py:62
  83.6 1.9 copy-done.1
  87.4 3.2 %fusion.40 = f32[4,32,512]{2,1,0:T(8,128)S(1)} fusion(bf16[512,4,32]{0,2,1:T(8,128)(2,1)S(1)} %bitcast.125, f32[4,512,512]{2,1,0:T(8,128)} %copy-done.1, f32[4,512]{1,0:T(4,128)S(1)} %get-tuple-element.380, pred[512]{0:T(512)(128)(4,1)S(1)} %dynamic-slice_reduce_fusion.5), kind=kOutput, calls=%fused_computation.7.clone.1 | convolution fusion | flops 72351744 | bytes 4596224 | tf_op jit(solution)/shard_map/while/body/eval_jaxpr/while/body/eval_jaxpr/hck,khd->chd/dot_general | solution.py:62
  93.6 1.4 fusion.34
  95.1 7.9 %dynamic_update_slice.30 = f32[4,512,128]{2,0,1:T(4,128)} dynamic-update-slice(f32[4,512,128]{2,0,1:T(4,128)} %get-tuple-element.425, f32[1,512,128]{2,0,1:T(1,128)S(1)} %copy.96, s32[]{:T(128)S(6)} %copy.121, s32[]{:T(128)} %constant.66.clone.1..sunk, s32[]{:T(128)} %constant.66.clone.1..sunk) | dynamic-update-slice | bytes 524292 | tf_op jit(solution)/shard_map/while/body/jit(dynamic_update_index_in_dim)/dynamic_update_slice | solution.py:87
  106.9 36.4 %while.30 = (s32[]{:T(128)}, f32[4,512,4]{1,2,0:T(4,128)}, f32[4,512,4]{1,2,0:T(4,128)}, f32[4,512,128]{1,2,0:T(8,128)}, pred[4,512]{1,0:T(4,128)(4,1)S(1)}, /*i...) while((s32[]{:T(128)}, f32[4,512,4]{1,2,0:T(4,128)}, ...), condition=%wide.region_5.5_spmd, body=%wide.region_2.4_spmd.sunk | while | flops 147845120 | bytes 31656596 | solution.py:70
  108.2 1.9 copy-done.1
  112.1 3.2 %fusion.40 = f32[4,32,512]{2,1,0:T(8,128)S(1)} fusion(bf16[512,4,32]{0,2,1:T(8,128)(2,1)S(1)} %bitcast.125, f32[4,512,512]{2,1,0:T(8,128)} %copy-done.1, f32[4,512]{1,0:T(4,128)S(1)} %get-tuple-element.380, pred[512]{0:T(512)(128)(4,1)S(1)} %dynamic-slice_reduce_fusion.5), kind=kOutput, calls=%fused_computation.7.clone.1 | convolution fusion | flops 72351744 | bytes 4596224 | tf_op jit(solution)/shard_map/while/body/eval_jaxpr/while/body/eval_jaxpr/hck,khd->chd/dot_general | solution.py:62
  117.3 1.9 copy-done.1
  121.1 3.2 %fusion.40 = f32[4,32,512]{2,1,0:T(8,128)S(1)} fusion(bf16[512,4,32]{0,2,1:T(8,128)(2,1)S(1)} %bitcast.125, f32[4,512,512]{2,1,0:T(8,128)} %copy-done.1, f32[4,512]{1,0:T(4,128)S(1)} %get-tuple-element.380, pred[512]{0:T(512)(128)(4,1)S(1)} %dynamic-slice_reduce_fusion.5), kind=kOutput, calls=%fused_computation.7.clone.1 | convolution fusion | flops 72351744 | bytes 4596224 | tf_op jit(solution)/shard_map/while/body/eval_jaxpr/while/body/eval_jaxpr/hck,khd->chd/dot_general | solution.py:62
  126.4 1.9 copy-done.1
  130.2 3.2 %fusion.40 = f32[4,32,512]{2,1,0:T(8,128)S(1)} fusion(bf16[512,4,32]{0,2,1:T(8,128)(2,1)S(1)} %bitcast.125, f32[4,512,512]{2,1,0:T(8,128)} %copy-done.1, f32[4,512]{1,0:T(4,128)S(1)} %get-tuple-element.380, pred[512]{0:T(512)(128)(4,1)S(1)} %dynamic-slice_reduce_fusion.5), kind=kOutput, calls=%fused_computation.7.clone.1 | convolution fusion | flops 72351744 | bytes 4596224 | tf_op jit(solution)/shard_map/while/body/eval_jaxpr/while/body/eval_jaxpr/hck,khd->chd/dot_general | solution.py:62
  135.5 1.9 copy-done.1
  139.3 3.2 %fusion.40 = f32[4,32,512]{2,1,0:T(8,128)S(1)} fusion(bf16[512,4,32]{0,2,1:T(8,128)(2,1)S(1)} %bitcast.125, f32[4,512,512]{2,1,0:T(8,128)} %copy-done.1, f32[4,512]{1,0:T(4,128)S(1)} %get-tuple-element.380, pred[512]{0:T(512)(128)(4,1)S(1)} %dynamic-slice_reduce_fusion.5), kind=kOutput, calls=%fused_computation.7.clone.1 | convolution fusion | flops 72351744 | bytes 4596224 | tf_op jit(solution)/shard_map/while/body/eval_jaxpr/while/body/eval_jaxpr/hck,khd->chd/dot_general | solution.py:62
  147.0 7.9 %dynamic_update_slice.30 = f32[4,512,128]{2,0,1:T(4,128)} dynamic-update-slice(f32[4,512,128]{2,0,1:T(4,128)} %get-tuple-element.425, f32[1,512,128]{2,0,1:T(1,128)S(1)} %copy.96, s32[]{:T(128)S(6)} %copy.121, s32[]{:T(128)} %constant.66.clone.1..sunk, s32[]{:T(128)} %constant.66.clone.1..sunk) | dynamic-update-slice | bytes 524292 | tf_op jit(solution)/shard_map/while/body/jit(dynamic_update_index_in_dim)/dynamic_update_slice | solution.py:87
  158.8 36.4 %while.30 = (s32[]{:T(128)}, f32[4,512,4]{1,2,0:T(4,128)}, f32[4,512,4]{1,2,0:T(4,128)}, f32[4,512,128]{1,2,0:T(8,128)}, pred[4,512]{1,0:T(4,128)(4,1)S(1)}, /*i...) while((s32[]{:T(128)}, f32[4,512,4]{1,2,0:T(4,128)}, ...), condition=%wide.region_5.5_spmd, body=%wide.region_2.4_spmd.sunk | while | flops 147845120 | bytes 31656596 | solution.py:70
  160.1 1.9 copy-done.1
  163.9 3.2 %fusion.40 = f32[4,32,512]{2,1,0:T(8,128)S(1)} fusion(bf16[512,4,32]{0,2,1:T(8,128)(2,1)S(1)} %bitcast.125, f32[4,512,512]{2,1,0:T(8,128)} %copy-done.1, f32[4,512]{1,0:T(4,128)S(1)} %get-tuple-element.380, pred[512]{0:T(512)(128)(4,1)S(1)} %dynamic-slice_reduce_fusion.5), kind=kOutput, calls=%fused_computation.7.clone.1 | convolution fusion | flops 72351744 | bytes 4596224 | tf_op jit(solution)/shard_map/while/body/eval_jaxpr/while/body/eval_jaxpr/hck,khd->chd/dot_general | solution.py:62
  169.2 1.9 copy-done.1
  173.0 3.2 %fusion.40 = f32[4,32,512]{2,1,0:T(8,128)S(1)} fusion(bf16[512,4,32]{0,2,1:T(8,128)(2,1)S(1)} %bitcast.125, f32[4,512,512]{2,1,0:T(8,128)} %copy-done.1, f32[4,512]{1,0:T(4,128)S(1)} %get-tuple-element.380, pred[512]{0:T(512)(128)(4,1)S(1)} %dynamic-slice_reduce_fusion.5), kind=kOutput, calls=%fused_computation.7.clone.1 | convolution fusion | flops 72351744 | bytes 4596224 | tf_op jit(solution)/shard_map/while/body/eval_jaxpr/while/body/eval_jaxpr/hck,khd->chd/dot_general | solution.py:62
  178.3 1.9 copy-done.1
  182.1 3.2 %fusion.40 = f32[4,32,512]{2,1,0:T(8,128)S(1)} fusion(bf16[512,4,32]{0,2,1:T(8,128)(2,1)S(1)} %bitcast.125, f32[4,512,512]{2,1,0:T(8,128)} %copy-done.1, f32[4,512]{1,0:T(4,128)S(1)} %get-tuple-element.380, pred[512]{0:T(512)(128)(4,1)S(1)} %dynamic-slice_reduce_fusion.5), kind=kOutput, calls=%fused_computation.7.clone.1 | convolution fusion | flops 72351744 | bytes 4596224 | tf_op jit(solution)/shard_map/while/body/eval_jaxpr/while/body/eval_jaxpr/hck,khd->chd/dot_general | solution.py:62
  187.4 1.9 copy-done.1
  191.2 3.2 %fusion.40 = f32[4,32,512]{2,1,0:T(8,128)S(1)} fusion(bf16[512,4,32]{0,2,1:T(8,128)(2,1)S(1)} %bitcast.125, f32[4,512,512]{2,1,0:T(8,128)} %copy-done.1, f32[4,512]{1,0:T(4,128)S(1)} %get-tuple-element.380, pred[512]{0:T(512)(128)(4,1)S(1)} %dynamic-slice_reduce_fusion.5), kind=kOutput, calls=%fused_computation.7.clone.1 | convolution fusion | flops 72351744 | bytes 4596224 | tf_op jit(solution)/shard_map/while/body/eval_jaxpr/while/body/eval_jaxpr/hck,khd->chd/dot_general | solution.py:62
  198.9 7.9 %dynamic_update_slice.30 = f32[4,512,128]{2,0,1:T(4,128)} dynamic-update-slice(f32[4,512,128]{2,0,1:T(4,128)} %get-tuple-element.425, f32[1,512,128]{2,0,1:T(1,128)S(1)} %copy.96, s32[]{:T(128)S(6)} %copy.121, s32[]{:T(128)} %constant.66.clone.1..sunk, s32[]{:T(128)} %constant.66.clone.1..sunk) | dynamic-update-slice | bytes 524292 | tf_op jit(solution)/shard_map/while/body/jit(dynamic_update_index_in_dim)/dynamic_update_slice | solution.py:87
  210.7 36.4 %while.30 = (s32[]{:T(128)}, f32[4,512,4]{1,2,0:T(4,128)}, f32[4,512,4]{1,2,0:T(4,128)}, f32[4,512,128]{1,2,0:T(8,128)}, pred[4,512]{1,0:T(4,128)(4,1)S(1)}, /*i...) while((s32[]{:T(128)}, f32[4,512,4]{1,2,0:T(4,128)}, ...), condition=%wide.region_5.5_spmd, body=%wide.region_2.4_spmd.sunk | while | flops 147845120 | bytes 31656596 | solution.py:70
  212.0 1.9 copy-done.1
  215.8 3.2 %fusion.40 = f32[4,32,512]{2,1,0:T(8,128)S(1)} fusion(bf16[512,4,32]{0,2,1:T(8,128)(2,1)S(1)} %bitcast.125, f32[4,512,512]{2,1,0:T(8,128)} %copy-done.1, f32[4,512]{1,0:T(4,128)S(1)} %get-tuple-element.380, pred[512]{0:T(512)(128)(4,1)S(1)} %dynamic-slice_reduce_fusion.5), kind=kOutput, calls=%fused_computation.7.clone.1 | convolution fusion | flops 72351744 | bytes 4596224 | tf_op jit(solution)/shard_map/while/body/eval_jaxpr/while/body/eval_jaxpr/hck,khd->chd/dot_general | solution.py:62
  221.1 1.9 copy-done.1
  224.9 3.2 %fusion.40 = f32[4,32,512]{2,1,0:T(8,128)S(1)} fusion(bf16[512,4,32]{0,2,1:T(8,128)(2,1)S(1)} %bitcast.125, f32[4,512,512]{2,1,0:T(8,128)} %copy-done.1, f32[4,512]{1,0:T(4,128)S(1)} %get-tuple-element.380, pred[512]{0:T(512)(128)(4,1)S(1)} %dynamic-slice_reduce_fusion.5), kind=kOutput, calls=%fused_computation.7.clone.1 | convolution fusion | flops 72351744 | bytes 4596224 | tf_op jit(solution)/shard_map/while/body/eval_jaxpr/while/body/eval_jaxpr/hck,khd->chd/dot_general | solution.py:62
  230.2 1.9 copy-done.1
  234.0 3.2 %fusion.40 = f32[4,32,512]{2,1,0:T(8,128)S(1)} fusion(bf16[512,4,32]{0,2,1:T(8,128)(2,1)S(1)} %bitcast.125, f32[4,512,512]{2,1,0:T(8,128)} %copy-done.1, f32[4,512]{1,0:T(4,128)S(1)} %get-tuple-element.380, pred[512]{0:T(512)(128)(4,1)S(1)} %dynamic-slice_reduce_fusion.5), kind=kOutput, calls=%fused_computation.7.clone.1 | convolution fusion | flops 72351744 | bytes 4596224 | tf_op jit(solution)/shard_map/while/body/eval_jaxpr/while/body/eval_jaxpr/hck,khd->chd/dot_general | solution.py:62
  239.3 1.9 copy-done.1
  243.1 3.2 %fusion.40 = f32[4,32,512]{2,1,0:T(8,128)S(1)} fusion(bf16[512,4,32]{0,2,1:T(8,128)(2,1)S(1)} %bitcast.125, f32[4,512,512]{2,1,0:T(8,128)} %copy-done.1, f32[4,512]{1,0:T(4,128)S(1)} %get-tuple-element.380, pred[512]{0:T(512)(128)(4,1)S(1)} %dynamic-slice_reduce_fusion.5), kind=kOutput, calls=%fused_computation.7.clone.1 | convolution fusion | flops 72351744 | bytes 4596224 | tf_op jit(solution)/shard_map/while/body/eval_jaxpr/while/body/eval_jaxpr/hck,khd->chd/dot_general | solution.py:62
  249.3 1.4 fusion.34
  250.8 7.9 %dynamic_update_slice.30 = f32[4,512,128]{2,0,1:T(4,128)} dynamic-update-slice(f32[4,512,128]{2,0,1:T(4,128)} %get-tuple-element.425, f32[1,512,128]{2,0,1:T(1,128)S(1)} %copy.96, s32[]{:T(128)S(6)} %copy.121, s32[]{:T(128)} %constant.66.clone.1..sunk, s32[]{:T(128)} %constant.66.clone.1..sunk) | dynamic-update-slice | bytes 524292 | tf_op jit(solution)/shard_map/while/body/jit(dynamic_update_index_in_dim)/dynamic_update_slice | solution.py:87
  258.6 2.1 copy.79
  260.8 2.3 bitcast_bitcast_fusion
  263.0 2.9 reshape.121
  266.0 8.7 %all-to-all-start.2 = ((f32[8,1,1024]{2,1,0:T(1,128)}), f32[8,1,1024]{2,1,0:T(1,128)S(1)}, u32[]{:S(2)}, u32[]{:S(2)}) async-start(f32[8,1,1024]{2,1,0:T(1,128)} %reshape.121), calls=%async_computation.2 | async-start | bytes 65536 | tf_op jit(solution)/shard_map/all_to_all | solution.py:90
  276.1 2.3 bitcast_bitcast_fusion.1
  278.4 2.3 reshape.119
  280.7 10.2 %all_to_all.51 = f32[8,1,1024]{2,1,0:T(1,128)S(1)} all-to-all(f32[8,1,1024]{2,1,0:T(1,128)S(1)} %reshape.119), channel_id=1, replica_groups=mesh['dp'=4,'hist'=8] {'hist'}, dimensions={0} | all-to-all | bytes 65536 | tf_op jit(solution)/shard_map/all_to_all | solution.py:89
  290.9 6.6 %all-to-all-start = ((f32[1,4,512,128]{3,1,0,2:T(4,128)}), f32[1,4,512,128]{3,1,0,2:T(4,128)}, u32[]{:S(2)}, u32[]{:S(2)}) async-start(f32[1,4,512,128]{3,1,0,2:T(4,128)} %bitcast.136), calls=%async_computation | async-start | bytes 2097152 | tf_op jit(solution)/shard_map/all_to_all | solution.py:91
  298.7 2.4 reshape.122
  301.8 2.4 reshape.120
  304.2 1.5 reduce_max.27
  305.6 3.1 multiply_reduce_fusion.1
  308.7 1.6 copy.77
  310.3 1.5 mul.55
  311.8 3.2 copy.78
  318.0 1.5 convolution_convert_fusion.2
  (248 shorter events, 98.5 us)
Async XLA Ops:
  0.0 5.8 %copy-start = (bf16[4,2048,128]{2,1,0:T(8,128)(2,1)S(1)}, bf16[4,2048,128]{2,1,0:T(8,128)(2,1)}, u32[]{:S(2)}) copy-start(bf16[4,2048,128]{2,1,0:T(8,128)(2,1)} %param.10) | copy-start | bytes 6291460
  5.8 43.1 %copy-start.2 = (bf16[4,128,128]{2,1,0:T(8,128)(2,1)}, bf16[4,128,128]{2,1,0:T(8,128)(2,1)S(1)}, u32[]{:S(2)}) copy-start(bf16[4,128,128]{2,1,0:T(8,128)(2,1)S(1)} %all_gather.6) | copy-start | bytes 393220
  15.5 4.5 %copy-start.3 = (bf16[4,64,128]{2,1,0:T(8,128)(2,1)S(1)}, bf16[4,64,128]{2,1,0:T(8,128)(2,1)}, u32[]{:S(2)}) copy-start(bf16[4,64,128]{2,1,0:T(8,128)(2,1)} %param.9) | copy-start | bytes 196612
  15.5 34.5 %copy-start.5 = (s32[4,64]{1,0:T(4,128)S(1)}, s32[4,64]{1,0:T(4,128)}, u32[]{:S(2)}) copy-start(s32[4,64]{1,0:T(4,128)} %param.13) | copy-start | bytes 3076
  15.5 34.9 %copy-start.6 = (s32[4]{0:T(128)S(1)}, s32[4]{0:T(128)}, u32[]{:S(2)}) copy-start(s32[4]{0:T(128)} %param.12) | copy-start | bytes 52
  56.3 1.9 copy-start.1
  65.4 1.9 copy-start.1
  74.5 1.9 copy-start.1
  83.6 1.9 copy-start.1
  108.2 1.9 copy-start.1
  117.3 1.9 copy-start.1
  126.4 1.9 copy-start.1
  135.5 1.9 copy-start.1
  160.1 1.9 copy-start.1
  169.2 1.9 copy-start.1
  178.3 1.9 copy-start.1
  187.4 1.9 copy-start.1
  212.0 1.9 copy-start.1
  221.1 1.9 copy-start.1
  230.2 1.9 copy-start.1
  239.3 1.9 copy-start.1
  258.6 16.1 %copy-start.4 = (f32[4,512,4]{1,2,0:T(4,128)S(1)}, f32[4,512,4]{1,2,0:T(4,128)}, u32[]{:S(2)}) copy-start(f32[4,512,4]{1,2,0:T(4,128)} %get-tuple-element.94) | copy-start | bytes 98308
  266.0 14.7 %all-to-all-start.2 = ((f32[8,1,1024]{2,1,0:T(1,128)}), f32[8,1,1024]{2,1,0:T(1,128)S(1)}, u32[]{:S(2)}, u32[]{:S(2)}) async-start(f32[8,1,1024]{2,1,0:T(1,128)} %reshape.121), calls=%async_computation.2 | async-start | bytes 65536 | tf_op jit(solution)/shard_map/all_to_all | solution.py:90
  290.9 24.4 %all-to-all-start = ((f32[1,4,512,128]{3,1,0,2:T(4,128)}), f32[1,4,512,128]{3,1,0,2:T(4,128)}, u32[]{:S(2)}, u32[]{:S(2)}) async-start(f32[1,4,512,128]{3,1,0,2:T(4,128)} %bitcast.136), calls=%async_computation | async-start | bytes 2097152 | tf_op jit(solution)/shard_map/all_to_all | solution.py:91
where the time goes:
time: 325 us; the launch traced here: 319 us
  local copies, waits for them, and re-layouts  144 us (44%)
  matrix products  75.4 us (23%)
  blocking collectives  44.8 us (14%)
  other arithmetic  38.9 us (12%)
  starting transfers between devices  15.3 us (5%)
    dynamic_update_slice x44, local copies, waits for them, and re-layouts, body(): maxima, totals, summed = lax.map(per_user, (queries, keys, values, live))  55.9 us
    dot_general x16, matrix products, one_piece(): jnp.einsum('hck,khd->chd', expo.astype(jnp.bfloat16), value_part.reshape(...  51.8 us
    while x32, local copies, waits for them, and re-layouts  30.7 us
    all_gather x1, blocking collectives, body(): whole = lax.all_gather(candidates, 'hist', axis=1, tiled=True)  28.9 us
    dynamic_slice x84, local copies, waits for them, and re-layouts, body(): maxima, totals, summed = lax.map(per_user, (queries, keys, values, live))  19.7 us
    reduce_sum x16, other arithmetic, one_piece(): totals = jnp.sum(expo, axis=-1)  18.6 us
    dot_general x16, matrix products, one_piece(): jnp.einsum('chd,khd->hck', query_heads, key_part.reshape(span, H, head_si...  17.7 us
    unnamed x18, local copies, waits for them, and re-layouts  14.6 us
  transfers between devices with their start and end apart: 2, of which 0 were waited for; matrix products, arithmetic and copies ran while one was open for 7% of the time, Pallas kernels for 0%

commit v1 on v0

v1 whole, which is shorter than its diff:
```python
import functools
import math

import jax
import jax.numpy as jnp
from jax import lax
from jax.experimental import pallas as pl
from jax.experimental.pallas import tpu as pltpu
from jax.sharding import PartitionSpec as P

H = 4
BLOCK = 128
PAIR = 2
LOW = -1e30


def attend_kernel(
    own_cands, lengths, selected, base, cand, hist, weights, parts, stats, qpad, acc, top, total, lse, live
):
    user = pl.program_id(0)
    users = pl.num_programs(0)
    cands, embed = cand.shape[1], cand.shape[2]
    head = embed // H
    factor = math.log2(math.e) / math.sqrt(head)
    blocks = hist.shape[1] // BLOCK
    length = lengths[user]
    first = base[0]
    chosen = selected.shape[1]

    def note(j, count):
        block = selected[user, j] - first
        live[count] = block
        ok = jnp.logical_and(block >= 0, block < blocks)
        ok = jnp.logical_and(ok, (block + first) * BLOCK < length)
        return count + jnp.where(ok, 1, 0)

    def note_many(j, count):
        for step in range(8):
            count = note(j * 8 + step, count)
        return count

    count = lax.fori_loop(0, chosen // 8, note_many, jnp.int32(0))

    query = lax.dot_general(
        weights[0], cand[0], (((0,), (1,)), ((), ())), preferred_element_type=jnp.float32
    ).astype(jnp.bfloat16)
    for h in range(H):
        rows = slice(h * head, (h + 1) * head)
        pieces = []
        if h > 0:
            pieces.append(jnp.zeros((h * head, cands), jnp.bfloat16))
        pieces.append(query[rows, :])
        if h < H - 1:
            pieces.append(jnp.zeros((embed - (h + 1) * head, cands), jnp.bfloat16))
        qpad[h] = jnp.concatenate(pieces, axis=0)
    acc[user] = jnp.zeros(acc.shape[1:], jnp.float32)
    top[...] = jnp.full(top.shape, LOW, jnp.float32)
    total[...] = jnp.zeros(total.shape, jnp.float32)

    @pl.loop(0, (count + PAIR - 1) // PAIR)
    def _(step):
        rows, biases = [], []
        places = lax.broadcasted_iota(jnp.int32, (BLOCK, 128), 0)
        for k in range(PAIR):
            at = step * PAIR + k
            inside = at < count
            block = jnp.where(inside, live[jnp.minimum(at, count - 1)], 0)
            limit = jnp.where(inside, length - (block + first) * BLOCK, 0)
            rows.append(hist[0, pl.ds(pl.multiple_of(block * BLOCK, BLOCK), BLOCK), :])
            biases.append(jnp.where(places < limit, 0.0, LOW))
        rows = jnp.concatenate(rows, axis=0)
        bias = jnp.concatenate(biases, axis=0)
        bias = jnp.concatenate([bias] * (cands // 128), axis=1)
        keys = jnp.dot(rows, weights[1], preferred_element_type=jnp.float32).astype(jnp.bfloat16)
        values = lax.dot_general(
            weights[2], rows, (((0,), (1,)), ((), ())), preferred_element_type=jnp.float32
        ).astype(jnp.bfloat16)
        for h in range(H):
            scores = jnp.dot(keys, qpad[h], preferred_element_type=jnp.float32) + bias
            before = top[h : h + 1, :]
            peak = jnp.maximum(before, jnp.max(scores, axis=0, keepdims=True))
            expo = jnp.exp2((scores - peak) * factor)
            shrink = jnp.exp2((before - peak) * factor)
            top[h : h + 1, :] = peak
            total[h : h + 1, :] = total[h : h + 1, :] * shrink + jnp.sum(expo, axis=0, keepdims=True)
            part = jnp.dot(
                values[h * head : (h + 1) * head, :],
                expo.astype(jnp.bfloat16),
                preferred_element_type=jnp.float32,
            )
            acc[user, h * head : (h + 1) * head, :] = acc[user, h * head : (h + 1) * head, :] * shrink + part

    for h in range(H):
        amount = total[h : h + 1, :]
        some = amount > 0.0
        safe = jnp.where(some, amount, 1.0)
        acc[user, h * head : (h + 1) * head, :] = acc[user, h * head : (h + 1) * head, :] * (1.0 / safe)
        lse[user, h : h + 1, :] = jnp.where(some, top[h : h + 1, :] * factor + jnp.log2(safe), LOW)

    @pl.when(user == users - 1)
    def _():
        for dest in range(parts.shape[0]):
            at = slice(dest * own_cands, (dest + 1) * own_cands)
            for u in range(acc.shape[0]):
                to = slice(u * own_cands, (u + 1) * own_cands)
                parts[dest, :, to] = acc[u, :, at].astype(jnp.bfloat16)
                stats[dest, :, to] = lse[u, :, at]


def combine_kernel(n, parts, stats, out_weight, result, got, got_stats, send_a, recv_a, send_b, recv_b):
    me = lax.axis_index("hist")
    barrier = pltpu.get_barrier_semaphore()
    for k in range(1, n):
        pl.semaphore_signal(
            barrier, inc=1, device_id={"hist": lax.rem(me + k, n)}, device_id_type=pl.DeviceIdType.MESH
        )
    pl.semaphore_wait(barrier, n - 1)
    copies = []
    for k in range(1, n):
        peer = lax.rem(me + k, n)
        for src, dst, send, recv in ((stats, got_stats, send_b, recv_b), (parts, got, send_a, recv_a)):
            copy = pltpu.make_async_remote_copy(
                src_ref=src.at[peer],
                dst_ref=dst.at[k - 1],
                send_sem=send.at[k - 1],
                recv_sem=recv.at[k - 1],
                device_id={"hist": peer},
                device_id_type=pl.DeviceIdType.MESH,
            )
            copy.start()
            copies.append(copy)
    for copy in copies:
        copy.wait()
    logs = [stats[me]] + [got_stats[k] for k in range(n - 1)]
    highest = functools.reduce(jnp.maximum, logs)
    shares = [jnp.exp2(log - highest) for log in logs]
    inverse = 1.0 / functools.reduce(jnp.add, shares)
    embed = parts.shape[1]
    head = embed // H
    pieces = []
    for h in range(H):
        rows = slice(h * head, (h + 1) * head)
        mixed = parts[me, rows, :].astype(jnp.float32) * shares[0][h : h + 1, :]
        for k in range(n - 1):
            mixed += got[k, rows, :].astype(jnp.float32) * shares[k + 1][h : h + 1, :]
        pieces.append(mixed * inverse[h : h + 1, :])
    attended = jnp.concatenate(pieces, axis=0).astype(jnp.bfloat16)
    result[...] = lax.dot_general(
        attended, out_weight[...], (((0,), (0,)), ((), ())), preferred_element_type=jnp.float32
    ).astype(jnp.bfloat16)


def body(candidates, history, projections, lengths, selected):
    n = lax.axis_size("hist")
    weights = lax.all_gather(projections, "dp", axis=1, tiled=True)
    whole = lax.all_gather(candidates, "hist", axis=1, tiled=True)
    users, own_cands, embed = candidates.shape
    cands = whole.shape[1]
    own_rows = history.shape[1]
    wide = -(-users * own_cands // 128) * 128
    base = (lax.axis_index("hist") * (own_rows // BLOCK)).astype(jnp.int32).reshape(1)
    parts, stats = pl.pallas_call(
        functools.partial(attend_kernel, own_cands),
        grid_spec=pltpu.PrefetchScalarGridSpec(
            num_scalar_prefetch=3,
            grid=(users,),
            in_specs=[
                pl.BlockSpec((1, cands, embed), lambda u, *_: (u, 0, 0)),
                pl.BlockSpec((1, own_rows, embed), lambda u, *_: (u, 0, 0)),
                pl.BlockSpec((4, embed, embed), lambda u, *_: (0, 0, 0)),
            ],
            out_specs=[
                pl.BlockSpec((n, embed, wide), lambda u, *_: (0, 0, 0)),
                pl.BlockSpec((n, H, wide), lambda u, *_: (0, 0, 0)),
            ],
            scratch_shapes=[
                pltpu.VMEM((H, embed, cands), jnp.bfloat16),
                pltpu.VMEM((users, embed, cands), jnp.float32),
                pltpu.VMEM((8, cands), jnp.float32),
                pltpu.VMEM((8, cands), jnp.float32),
                pltpu.VMEM((users, H, cands), jnp.float32),
                pltpu.SMEM((selected.shape[1] + 8,), jnp.int32),
            ],
        ),
        out_shape=[
            jax.ShapeDtypeStruct((n, embed, wide), jnp.bfloat16),
            jax.ShapeDtypeStruct((n, H, wide), jnp.float32),
        ],
        name="attend",
    )(lengths, selected, base, whole, history, weights)
    result = pl.pallas_call(
        functools.partial(combine_kernel, n),
        out_shape=jax.ShapeDtypeStruct((wide, embed), jnp.bfloat16),
        in_specs=[pl.BlockSpec(memory_space=pltpu.VMEM)] * 3,
        out_specs=pl.BlockSpec(memory_space=pltpu.VMEM),
        scratch_shapes=[
            pltpu.VMEM((n - 1, embed, wide), jnp.bfloat16),
            pltpu.VMEM((n - 1, H, wide), jnp.float32),
        ]
        + [pltpu.SemaphoreType.DMA((n - 1,))] * 4,
        compiler_params=pltpu.CompilerParams(collective_id=0, has_side_effects=True),
        name="combine",
    )(parts, stats, weights[3])
    return result[: users * own_cands].reshape(users, own_cands, embed)


def solution(mesh):
    placed = (
        P("dp", "hist", None),
        P("dp", "hist", None),
        P(None, "dp", None),
        P("dp"),
        P("dp", None),
    )
    return jax.shard_map(
        body, mesh=mesh, in_specs=placed, out_specs=P("dp", "hist", None), check_vma=False
    )
```

time: 325 us -> 90.5 us (0.28); the launches traced: 319 us -> 89.6 us
  local copies, waits for them, and re-layouts: 144 us -> 2.85 us
  matrix products: 75.4 us -> 0 us
  Pallas kernels: 0 us -> 48.5 us
  other arithmetic: 38.9 us -> 0 us
  starting transfers between devices: 15.3 us -> 0 us
  blocking collectives: 44.8 us -> 38.2 us
    dot_general x35 -> x0, matrix products: 75.4 us -> none  [the longest x16 51.8 us: one_piece(): jnp.einsum('hck,khd->chd', expo.astype(jnp.bfloat16), value_part.reshape(...]
    dynamic_update_slice x44 -> x0, local copies, waits for them, and re-layouts: 55.9 us -> none  [body(): maxima, totals, summed = lax.map(per_user, (queries, keys, values, live))]
    pallas_call x0 -> x2, Pallas kernels: none -> 48.5 us  [the longest x1 30 us: body(): pl.pallas_call(functools.partial(attend_kernel, own_cands), grid_spec=plt...]
    while x34 -> x0, local copies, waits for them, and re-layouts: 34.2 us -> none
    reduce_sum x26 -> x0, other arithmetic: 31.7 us -> none  [the longest x16 18.6 us: one_piece(): totals = jnp.sum(expo, axis=-1)]
    dynamic_slice x100 -> x0, local copies, waits for them, and re-layouts: 20.1 us -> none  [the longest x84 19.7 us: body(): maxima, totals, summed = lax.map(per_user, (queries, keys, values, live))]
    all_to_all x2 -> x0, starting transfers between devices: 15.3 us -> none  [the longest x1 8.73 us: body(): lax.all_to_all(totals[None], 'hist', split_axis=2, concat_axis=0, tiled=T...]
    unnamed x18 -> x1, local copies, waits for them, and re-layouts: 14.6 us -> 1.47 us
  transfers between devices with their start and end apart: 2 -> 0, of which waited for: 0 -> 0; matrix products, arithmetic and copies ran while one was open for 7% -> 0% of each run, Pallas kernels for 0% -> 0%
where the time goes in v1:
time: 90.5 us; the launch traced here: 89.6 us
  Pallas kernels  48.5 us (54%)
  blocking collectives  38.2 us (42%)
  local copies, waits for them, and re-layouts  2.85 us (3%)
    all_gather x1, blocking collectives, body(): whole = lax.all_gather(candidates, 'hist', axis=1, tiled=True)  31.2 us
    pallas_call x1, Pallas kernels, body(): pl.pallas_call(functools.partial(attend_kernel, own_cands), grid_spec=plt...  30 us
    pallas_call x1, Pallas kernels, body(): pl.pallas_call(functools.partial(combine_kernel, n), out_shape=jax.ShapeD...  18.5 us
    all_gather x1, blocking collectives, body(): weights = lax.all_gather(projections, 'dp', axis=1, tiled=True)  6.92 us

profile of v1, /device:TPU:12, one launch (start us, length us, event | category | flops | bytes accessed | tf_op | source)
XLA Modules:
  0.0 89.6 jit_solution(142078153882617042)
XLA Ops:
  0.0 6.9 %all_gather.7.weights = bf16[4,128,128]{2,1,0:T(8,128)(2,1)} all-gather(bf16[4,32,128]{2,1,0:T(8,128)(2,1)} %param.7), channel_id=1, replica_groups=mesh['dp'=4,'hist'=8] {'dp'}, dimensions={1}, use_global_device_ids=true | all-gather | bytes 163840 | tf_op jit(solution)/shard_map/all_gather | solution.py:155
  6.9 31.2 %all_gather.6.cand = bf16[4,512,128]{2,1,0:T(8,128)(2,1)} all-gather(bf16[4,64,128]{2,1,0:T(8,128)(2,1)} %param.5), channel_id=1, replica_groups=mesh['dp'=4,'hist'=8] {'hist'}, dimensions={1}, use_global_device_ids=true | all-gather | bytes 589824 | tf_op jit(solution)/shard_map/all_gather | solution.py:156
  38.2 30.0 %attend.1 = (bf16[8,128,256]{2,1,0:T(8,128)(2,1)}, f32[8,4,256]{2,1,0:T(4,128)}) custom-call(s32[4]{0:T(128)} %lengths.1, s32[4,64]{1,0:T(4,128)} %selected.1, s32[1]{0:T(128)} %bitcast.base, bf16[4,512,128]{2,1,0:T(8,128)(2,1)} %all_gather.6.cand, bf16[4,2048,128]{2,1,0:T(8,128)(2,1)} %hist.1, bf16[4,128,128]{2,1,0:T(8,128)(2,1)} %all_gather.7.weights), custom_call_target="tpu_custom_call" | custom-call | tf_op jit(solution)/shard_map/attend/pallas_call | solution.py:162
  68.2 1.4 %slice_bitcast_fusion.out_weight = bf16[128,128]{1,0:T(8,128)(2,1)} fusion(bf16[4,128,128]{2,1,0:T(8,128)(2,1)} %all_gather.7.weights), kind=kLoop, calls=%fused_computation | loop fusion | bytes 65536 | tf_op jit(solution)/shard_map/squeeze | solution.py:203
  69.5 18.5 %combine.1 = bf16[256,128]{1,0:T(8,128)(2,1)} custom-call(bf16[8,128,256]{2,1,0:T(8,128)(2,1)} %get-tuple-element.7.parts, f32[8,4,256]{2,1,0:T(4,128)} %get-tuple-element.8.stats, bf16[128,128]{1,0:T(8,128)(2,1)} %slice_bitcast_fusion.out_weight), custom_call_target="tpu_custom_call" | custom-call | tf_op jit(solution)/shard_map/combine/pallas_call | solution.py:191
  88.1 1.5 %copy.7 = bf16[4,64,128]{2,1,0:T(8,128)(2,1)} copy(bf16[4,64,128]{2,1,0:T(8,128)(2,1)} %bitcast.4) | data formatting | bytes 131072

commit v2 on v1

--- a/solution.py
+++ b/solution.py
@@ -14,13 +14,108 @@
 LOW = -1e30
 
 
+def gather_kernel(
+    n, ranks, cand, proj, all_cand, all_proj, own_sem, z_send, z_recv, y_send, y_recv, w_send, w_recv
+):
+    mesh_id = pl.DeviceIdType.MESH
+    me, rank = lax.axis_index("hist"), lax.axis_index("dp")
+    line = n // 2
+    side, spot = lax.rem(me, 2), me // 2
+    users, own = cand.shape[0], cand.shape[1]
+    rows = proj.shape[1]
+    partner = spot * 2 + (1 - side)
+    peers = [lax.rem(spot + k, line) * 2 + side for k in range(1, line)]
+    mates = [lax.rem(rank + k, ranks) for k in range(1, ranks)]
+
+    barrier = pltpu.get_barrier_semaphore()
+    for peer in [partner] + peers:
+        pl.semaphore_signal(barrier, inc=1, device_id={"hist": peer}, device_id_type=mesh_id)
+    for mate in mates:
+        pl.semaphore_signal(barrier, inc=1, device_id={"dp": mate}, device_id_type=mesh_id)
+    pl.semaphore_wait(barrier, line + ranks - 1)
+
+    def place(u, owner):
+        return all_cand.at[u, pl.ds(pl.multiple_of(owner * own, own), own), :]
+
+    strip = all_proj.at[:, pl.ds(pl.multiple_of(rank * rows, rows), rows), :]
+    weight_copies = []
+    for k, mate in enumerate(mates):
+        copy = pltpu.make_async_remote_copy(
+            proj, strip, w_send.at[k], w_recv.at[k], device_id={"dp": mate}, device_id_type=mesh_id
+        )
+        copy.start()
+        weight_copies.append(copy)
+    across, along = [], {}
+    for u in range(users):
+        for k, peer in enumerate(peers):
+            copy = pltpu.make_async_remote_copy(
+                cand.at[u],
+                place(u, me),
+                z_send.at[k, u],
+                z_recv.at[k, u],
+                device_id={"hist": peer},
+                device_id_type=mesh_id,
+            )
+            copy.start()
+            along[k, u] = copy
+        copy = pltpu.make_async_remote_copy(
+            cand.at[u],
+            place(u, me),
+            y_send.at[0, u],
+            y_recv.at[0, u],
+            device_id={"hist": partner},
+            device_id_type=mesh_id,
+        )
+        copy.start()
+        across.append(copy)
+    locals_ = [pltpu.make_async_copy(proj, strip, own_sem.at[users])]
+    locals_ += [pltpu.make_async_copy(cand.at[u], place(u, me), own_sem.at[u]) for u in range(users)]
+    for copy in locals_:
+        copy.start()
+    for u in range(users):
+        for k in range(line - 1):
+            along[k, u].wait_recv()
+            source = lax.rem(spot + line - (k + 1), line) * 2 + side
+            copy = pltpu.make_async_remote_copy(
+                place(u, source),
+                place(u, source),
+                y_send.at[k + 1, u],
+                y_recv.at[k + 1, u],
+                device_id={"hist": partner},
+                device_id_type=mesh_id,
+            )
+            copy.start()
+            across.append(copy)
+    for copy in along.values():
+        copy.wait_send()
+    for copy in across + weight_copies + locals_:
+        copy.wait()
+
+
 def attend_kernel(
-    own_cands, lengths, selected, base, cand, hist, weights, parts, stats, qpad, acc, top, total, lse, live
+    own_cands,
+    lengths,
+    selected,
+    base,
+    cand,
+    hist,
+    weights,
+    parts,
+    stats,
+    qpad,
+    keys,
+    values,
+    acc,
+    top,
+    mean,
+    lse,
+    live,
 ):
     user = pl.program_id(0)
     users = pl.num_programs(0)
     cands, embed = cand.shape[1], cand.shape[2]
     head = embed // H
+    tall = values.shape[1]
     factor = math.log2(math.e) / math.sqrt(head)
     blocks = hist.shape[1] // BLOCK
     length = lengths[user]
@@ -53,57 +148,60 @@
         if h < H - 1:
             pieces.append(jnp.zeros((embed - (h + 1) * head, cands), jnp.bfloat16))
         qpad[h] = jnp.concatenate(pieces, axis=0)
-    acc[user] = jnp.zeros(acc.shape[1:], jnp.float32)
+    down = lax.broadcasted_iota(jnp.int32, (BLOCK, embed), 0)
+    right = lax.broadcasted_iota(jnp.int32, (tall - head, BLOCK), 1)
+    under = lax.broadcasted_iota(jnp.int32, (tall - head, BLOCK), 0)
+    for b in range(blocks):
+        limit = length - (first + b) * BLOCK
+        span = slice(b * BLOCK, (b + 1) * BLOCK)
+        rows = hist[0, span, :]
+        alive = down < limit
+        safe = jnp.where(alive, rows.astype(jnp.float32), rows[0:1, :].astype(jnp.float32)).astype(jnp.bfloat16)
+        kept = jnp.where(alive, rows.astype(jnp.float32), 0.0).astype(jnp.bfloat16)
+        keys[span, :] = jnp.dot(safe, weights[1], preferred_element_type=jnp.float32).astype(jnp.bfloat16)
+        turned = lax.dot_general(
+            weights[2], kept, (((0,), (1,)), ((), ())), preferred_element_type=jnp.float32
+        ).astype(jnp.bfloat16)
+        ones = jnp.where(jnp.logical_and(right < limit, under == 0), 1.0, 0.0).astype(jnp.bfloat16)
+        for h in range(H):
+            values[h, 0:head, span] = turned[h * head : (h + 1) * head, :]
+            values[h, head:tall, span] = ones
+    acc[...] = jnp.zeros(acc.shape, jnp.float32)
     top[...] = jnp.full(top.shape, LOW, jnp.float32)
-    total[...] = jnp.zeros(total.shape, jnp.float32)
 
     @pl.loop(0, (count + PAIR - 1) // PAIR)
     def _(step):
-        rows, biases = [], []
-        places = lax.broadcasted_iota(jnp.int32, (BLOCK, 128), 0)
+        starts, flags = [], []
         for k in range(PAIR):
             at = step * PAIR + k
-            inside = at < count
-            block = jnp.where(inside, live[jnp.minimum(at, count - 1)], 0)
-            limit = jnp.where(inside, length - (block + first) * BLOCK, 0)
-            rows.append(hist[0, pl.ds(pl.multiple_of(block * BLOCK, BLOCK), BLOCK), :])
-            biases.append(jnp.where(places < limit, 0.0, LOW))
-        rows = jnp.concatenate(rows, axis=0)
-        bias = jnp.concatenate(biases, axis=0)
-        bias = jnp.concatenate([bias] * (cands // 128), axis=1)
-        keys = jnp.dot(rows, weights[1], preferred_element_type=jnp.float32).astype(jnp.bfloat16)
-        values = lax.dot_general(
-            weights[2], rows, (((0,), (1,)), ((), ())), preferred_element_type=jnp.float32
-        ).astype(jnp.bfloat16)
+            block = live[jnp.minimum(at, count - 1)]
+            starts.append(pl.ds(pl.multiple_of(block * BLOCK, BLOCK), BLOCK))
+            flags.append(jnp.where(at < count, 1.0, 0.0).astype(jnp.bfloat16))
+        key = jnp.concatenate([keys[at, :] for at in starts], axis=0)
         for h in range(H):
-            scores = jnp.dot(keys, qpad[h], preferred_element_type=jnp.float32) + bias
+            scores = jnp.dot(key, qpad[h], preferred_element_type=jnp.float32)
             before = top[h : h + 1, :]
             peak = jnp.maximum(before, jnp.max(scores, axis=0, keepdims=True))
-            expo = jnp.exp2((scores - peak) * factor)
+            expo = jnp.exp2((scores - peak) * factor).astype(jnp.bfloat16)
             shrink = jnp.exp2((before - peak) * factor)
             top[h : h + 1, :] = peak
-            total[h : h + 1, :] = total[h : h + 1, :] * shrink + jnp.sum(expo, axis=0, keepdims=True)
-            part = jnp.dot(
-                values[h * head : (h + 1) * head, :],
-                expo.astype(jnp.bfloat16),
-                preferred_element_type=jnp.float32,
-            )
-            acc[user, h * head : (h + 1) * head, :] = acc[user, h * head : (h + 1) * head, :] * shrink + part
+            value = jnp.concatenate([values[h, :, at] * flag for at, flag in zip(starts, flags)], axis=1)
+            acc[h] = acc[h] * shrink + jnp.dot(value, expo, preferred_element_type=jnp.float32)
 
     for h in range(H):
-        amount = total[h : h + 1, :]
+        amount = acc[h, head : head + 1, :]
         some = amount > 0.0
         safe = jnp.where(some, amount, 1.0)
-        acc[user, h * head : (h + 1) * head, :] = acc[user, h * head : (h + 1) * head, :] * (1.0 / safe)
+        mean[user, h * head : (h + 1) * head, :] = (acc[h, 0:head, :] * (1.0 / safe)).astype(jnp.bfloat16)
         lse[user, h : h + 1, :] = jnp.where(some, top[h : h + 1, :] * factor + jnp.log2(safe), LOW)
 
     @pl.when(user == users - 1)
     def _():
         for dest in range(parts.shape[0]):
             at = slice(dest * own_cands, (dest + 1) * own_cands)
-            for u in range(acc.shape[0]):
+            for u in range(mean.shape[0]):
                 to = slice(u * own_cands, (u + 1) * own_cands)
-                parts[dest, :, to] = acc[u, :, at].astype(jnp.bfloat16)
+                parts[dest, :, to] = mean[u, :, at]
                 stats[dest, :, to] = lse[u, :, at]
 
 
@@ -146,16 +244,36 @@
         pieces.append(mixed * inverse[h : h + 1, :])
     attended = jnp.concatenate(pieces, axis=0).astype(jnp.bfloat16)
     result[...] = lax.dot_general(
-        attended, out_weight[...], (((0,), (0,)), ((), ())), preferred_element_type=jnp.float32
+        attended, out_weight[3], (((0,), (0,)), ((), ())), preferred_element_type=jnp.float32
     ).astype(jnp.bfloat16)
 
 
 def body(candidates, history, projections, lengths, selected):
     n = lax.axis_size("hist")
-    weights = lax.all_gather(projections, "dp", axis=1, tiled=True)
-    whole = lax.all_gather(candidates, "hist", axis=1, tiled=True)
+    ranks = lax.axis_size("dp")
     users, own_cands, embed = candidates.shape
-    cands = whole.shape[1]
+    cands = n * own_cands
+    line = n // 2
+    whole, weights = pl.pallas_call(
+        functools.partial(gather_kernel, n, ranks),
+        out_shape=[
+            jax.ShapeDtypeStruct((users, cands, embed), jnp.bfloat16),
+            jax.ShapeDtypeStruct((projections.shape[0], ranks * projections.shape[1], embed), jnp.bfloat16),
+        ],
+        in_specs=[pl.BlockSpec(memory_space=pltpu.VMEM)] * 2,
+        out_specs=[pl.BlockSpec(memory_space=pltpu.VMEM)] * 2,
+        scratch_shapes=[
+            pltpu.SemaphoreType.DMA((users + 1,)),
+            pltpu.SemaphoreType.DMA((line - 1, users)),
+            pltpu.SemaphoreType.DMA((line - 1, users)),
+            pltpu.SemaphoreType.DMA((line, users)),
+            pltpu.SemaphoreType.DMA((line, users)),
+            pltpu.SemaphoreType.DMA((ranks - 1,)),
+            pltpu.SemaphoreType.DMA((ranks - 1,)),
+        ],
+        compiler_params=pltpu.CompilerParams(collective_id=1, has_side_effects=True),
+        name="gather",
+    )(candidates, projections)
     own_rows = history.shape[1]
     wide = -(-users * own_cands // 128) * 128
     base = (lax.axis_index("hist") * (own_rows // BLOCK)).astype(jnp.int32).reshape(1)
@@ -175,9 +293,11 @@
             ],
             scratch_shapes=[
                 pltpu.VMEM((H, embed, cands), jnp.bfloat16),
-                pltpu.VMEM((users, embed, cands), jnp.float32),
+                pltpu.VMEM((own_rows, embed), jnp.bfloat16),
+                pltpu.VMEM((H, embed // H + 16, own_rows), jnp.bfloat16),
+                pltpu.VMEM((H, embed // H + 16, cands), jnp.float32),
                 pltpu.VMEM((8, cands), jnp.float32),
-                pltpu.VMEM((8, cands), jnp.float32),
+                pltpu.VMEM((users, embed, cands), jnp.bfloat16),
                 pltpu.VMEM((users, H, cands), jnp.float32),
                 pltpu.SMEM((selected.shape[1] + 8,), jnp.int32),
             ],
@@ -200,7 +320,7 @@
         + [pltpu.SemaphoreType.DMA((n - 1,))] * 4,
         compiler_params=pltpu.CompilerParams(collective_id=0, has_side_effects=True),
         name="combine",
-    )(parts, stats, weights[3])
+    )(parts, stats, weights)
     return result[: users * own_cands].reshape(users, own_cands, embed)
 
 

time: 90.5 us -> 67.3 us (0.74)
  blocking collectives: 38.2 us -> 0 us
  Pallas kernels: 48.5 us -> 64.6 us
  local copies, waits for them, and re-layouts: 2.85 us -> 1.47 us
    all_gather x2 -> x0, blocking collectives: 38.2 us -> none  [the longest x1 31.2 us: body(): whole = lax.all_gather(candidates, 'hist', axis=1, tiled=True)]
    pallas_call x0 -> x1, Pallas kernels: none -> 14.3 us  [body(): pl.pallas_call(functools.partial(gather_kernel, n, ranks), out_shape=[jax...]
    squeeze x1 -> x0, local copies, waits for them, and re-layouts: 1.38 us -> none  [body(): weights[3]]
    pallas_call x1, Pallas kernels: 18.5 us -> 19.9 us  [body(): pl.pallas_call(functools.partial(combine_kernel, n), out_shape=jax.ShapeD...]
where the time goes in v2:
time: 67.3 us; the launch traced here: 66.1 us
  Pallas kernels  64.6 us (96%)
  local copies, waits for them, and re-layouts  1.47 us (2%)
    pallas_call x1, Pallas kernels, body(): pl.pallas_call(functools.partial(attend_kernel, own_cands), grid_spec=plt...  30.4 us
    pallas_call x1, Pallas kernels, body(): pl.pallas_call(functools.partial(combine_kernel, n), out_shape=jax.ShapeD...  19.9 us
    pallas_call x1, Pallas kernels, body(): pl.pallas_call(functools.partial(gather_kernel, n, ranks), out_shape=[jax...  14.3 us
    unnamed x1, local copies, waits for them, and re-layouts  1.47 us

profile of v2, /device:TPU:12, one launch (start us, length us, event | category | flops | bytes accessed | tf_op | source)
XLA Modules:
  0.0 66.1 jit_solution(11025461561674413185)
XLA Ops:
  0.0 14.3 %gather.1 = (bf16[4,512,128]{2,1,0:T(8,128)(2,1)}, bf16[4,128,128]{2,1,0:T(8,128)(2,1)}) custom-call(bf16[4,64,128]{2,1,0:T(8,128)(2,1)} %cand.1, bf16[4,32,128]{2,1,0:T(8,128)(2,1)} %proj.1), custom_call_target="tpu_custom_call" | custom-call | tf_op jit(solution)/shard_map/gather/pallas_call | solution.py:257
  14.3 30.4 %attend.1 = (bf16[8,128,256]{2,1,0:T(8,128)(2,1)}, f32[8,4,256]{2,1,0:T(4,128)}) custom-call(s32[4]{0:T(128)} %lengths.1, s32[4,64]{1,0:T(4,128)} %selected.1, s32[1]{0:T(128)} %bitcast.base, bf16[4,512,128]{2,1,0:T(8,128)(2,1)} %get-tuple-element.9.cand, bf16[4,2048,128]{2,1,0:T(8,128)(2,1)} %hist.1, bf16[4,128,128]{2,1,0:T(8,128)(2,1)} %get-tuple-element.10.weights.out_weight), custom_call_target="tpu_custom_call" | custom-call | tf_op jit(solution)/shard_map/attend/pallas_call | solution.py:280
  44.8 19.9 %combine.1 = bf16[256,128]{1,0:T(8,128)(2,1)} custom-call(bf16[8,128,256]{2,1,0:T(8,128)(2,1)} %get-tuple-element.11.parts, f32[8,4,256]{2,1,0:T(4,128)} %get-tuple-element.12.stats, bf16[4,128,128]{2,1,0:T(8,128)(2,1)} %get-tuple-element.10.weights.out_weight), custom_call_target="tpu_custom_call" | custom-call | tf_op jit(solution)/shard_map/combine/pallas_call | solution.py:311
  64.6 1.5 %copy.7 = bf16[4,64,128]{2,1,0:T(8,128)(2,1)} copy(bf16[4,64,128]{2,1,0:T(8,128)(2,1)} %bitcast.2) | data formatting | bytes 131072

commit v3 on v2

--- a/solution.py
+++ b/solution.py
@@ -15,7 +15,28 @@
 
 
 def gather_kernel(
-    n, ranks, cand, proj, all_cand, all_proj, own_sem, z_send, z_recv, y_send, y_recv, w_send, w_recv
+    n,
+    ranks,
+    lengths,
+    cand,
+    proj,
+    hist,
+    all_cand,
+    all_proj,
+    all_keys,
+    all_values,
+    rows_in,
+    keys,
+    values,
+    own_sem,
+    in_sem,
+    out_sem,
+    z_send,
+    z_recv,
+    y_send,
+    y_recv,
+    w_send,
+    w_recv,
 ):
     mesh_id = pl.DeviceIdType.MESH
     me, rank = lax.axis_index("hist"), lax.axis_index("dp")
@@ -23,6 +44,11 @@
     side, spot = lax.rem(me, 2), me // 2
     users, own = cand.shape[0], cand.shape[1]
     rows = proj.shape[1]
+    own_rows, embed = hist.shape[1], hist.shape[2]
+    blocks = own_rows // BLOCK
+    fetches = [pltpu.make_async_copy(hist.at[u], rows_in.at[u], in_sem.at[u]) for u in range(users)]
+    for copy in fetches:
+        copy.start()
     partner = spot * 2 + (1 - side)
     peers = [lax.rem(spot + k, line) * 2 + side for k in range(1, line)]
     mates = [lax.rem(rank + k, ranks) for k in range(1, ranks)]
@@ -72,6 +98,14 @@
     locals_ += [pltpu.make_async_copy(cand.at[u], place(u, me), own_sem.at[u]) for u in range(users)]
     for copy in locals_:
         copy.start()
+    locals_[0].wait()
+    for copy in weight_copies:
+        copy.wait()
+    key_weight, value_weight = all_proj[1], all_proj[2]
+    shape = (blocks, BLOCK, embed)
+    places = lax.broadcasted_iota(jnp.int32, shape, 0) * BLOCK + lax.broadcasted_iota(jnp.int32, shape, 1)
+    places = places + me * own_rows
+    stores = []
     for u in range(users):
         for k in range(line - 1):
             along[k, u].wait_recv()
@@ -86,25 +120,37 @@
             )
             copy.start()
             across.append(copy)
+        fetches[u].wait()
+        block_rows = rows_in[u].reshape(shape).astype(jnp.float32)
+        alive = places < lengths[u]
+        safe = jnp.where(alive, block_rows, block_rows[:, 0:1, :]).astype(jnp.bfloat16).reshape(own_rows, embed)
+        kept = jnp.where(alive, block_rows, 0.0).astype(jnp.bfloat16).reshape(own_rows, embed)
+        keys[u] = jnp.dot(safe, key_weight, preferred_element_type=jnp.float32).astype(jnp.bfloat16)
+        values[u] = lax.dot_general(
+            value_weight, kept, (((0,), (1,)), ((), ())), preferred_element_type=jnp.float32
+        ).astype(jnp.bfloat16)
+        for k, (src, dst) in enumerate(((keys, all_keys), (values, all_values))):
+            copy = pltpu.make_async_copy(src.at[u], dst.at[u], out_sem.at[k, u])
+            copy.start()
+            stores.append(copy)
     for copy in along.values():
         copy.wait_send()
-    for copy in across + weight_copies + locals_:
+    for copy in across + locals_[1:] + stores:
         copy.wait()
 
 
 def attend_kernel(
     own_cands,
     lengths,
-    selected,
+    flags,
     base,
     cand,
-    hist,
+    keys,
+    values,
     weights,
     parts,
     stats,
     qpad,
-    keys,
-    values,
     acc,
     top,
     mean,
@@ -115,26 +161,14 @@
     users = pl.num_programs(0)
     cands, embed = cand.shape[1], cand.shape[2]
     head = embed // H
-    tall = values.shape[1]
+    tall = acc.shape[1]
     factor = math.log2(math.e) / math.sqrt(head)
-    blocks = hist.shape[1] // BLOCK
     length = lengths[user]
     first = base[0]
-    chosen = selected.shape[1]
-
-    def note(j, count):
-        block = selected[user, j] - first
-        live[count] = block
-        ok = jnp.logical_and(block >= 0, block < blocks)
-        ok = jnp.logical_and(ok, (block + first) * BLOCK < length)
-        return count + jnp.where(ok, 1, 0)
-
-    def note_many(j, count):
-        for step in range(8):
-            count = note(j * 8 + step, count)
-        return count
-
-    count = lax.fori_loop(0, chosen // 8, note_many, jnp.int32(0))
+    count = jnp.int32(0)
+    for b in range(keys.shape[1] // BLOCK):
+        live[count] = b
+        count = count + flags[user, b]
 
     query = lax.dot_general(
         weights[0], cand[0], (((0,), (1,)), ((), ())), preferred_element_type=jnp.float32
@@ -148,36 +182,21 @@
         if h < H - 1:
             pieces.append(jnp.zeros((embed - (h + 1) * head, cands), jnp.bfloat16))
         qpad[h] = jnp.concatenate(pieces, axis=0)
-    down = lax.broadcasted_iota(jnp.int32, (BLOCK, embed), 0)
+    acc[...] = jnp.zeros(acc.shape, jnp.float32)
+    top[...] = jnp.full(top.shape, LOW, jnp.float32)
+
     right = lax.broadcasted_iota(jnp.int32, (tall - head, BLOCK), 1)
     under = lax.broadcasted_iota(jnp.int32, (tall - head, BLOCK), 0)
-    for b in range(blocks):
-        limit = length - (first + b) * BLOCK
-        span = slice(b * BLOCK, (b + 1) * BLOCK)
-        rows = hist[0, span, :]
-        alive = down < limit
-        safe = jnp.where(alive, rows.astype(jnp.float32), rows[0:1, :].astype(jnp.float32)).astype(jnp.bfloat16)
-        kept = jnp.where(alive, rows.astype(jnp.float32), 0.0).astype(jnp.bfloat16)
-        keys[span, :] = jnp.dot(safe, weights[1], preferred_element_type=jnp.float32).astype(jnp.bfloat16)
-        turned = lax.dot_general(
-            weights[2], kept, (((0,), (1,)), ((), ())), preferred_element_type=jnp.float32
-        ).astype(jnp.bfloat16)
-        ones = jnp.where(jnp.logical_and(right < limit, under == 0), 1.0, 0.0).astype(jnp.bfloat16)
-        for h in range(H):
-            values[h, 0:head, span] = turned[h * head : (h + 1) * head, :]
-            values[h, head:tall, span] = ones
-    acc[...] = jnp.zeros(acc.shape, jnp.float32)
-    top[...] = jnp.full(top.shape, LOW, jnp.float32)
-
-    @pl.loop(0, (count + PAIR - 1) // PAIR)
-    def _(step):
-        starts, flags = [], []
-        for k in range(PAIR):
-            at = step * PAIR + k
-            block = live[jnp.minimum(at, count - 1)]
+    right = jnp.where(under == 0, right, jnp.iinfo(jnp.int32).max)
+
+    def visit(begin, many):
+        starts, ones = [], []
+        for k in range(many):
+            block = live[begin + k]
             starts.append(pl.ds(pl.multiple_of(block * BLOCK, BLOCK), BLOCK))
-            flags.append(jnp.where(at < count, 1.0, 0.0).astype(jnp.bfloat16))
-        key = jnp.concatenate([keys[at, :] for at in starts], axis=0)
+            ones.append(jnp.where(right < length - (block + first) * BLOCK, 1.0, 0.0).astype(jnp.bfloat16))
+        key = jnp.concatenate([keys[0, at, :] for at in starts], axis=0)
+        one = jnp.concatenate(ones, axis=1)
         for h in range(H):
             scores = jnp.dot(key, qpad[h], preferred_element_type=jnp.float32)
             before = top[h : h + 1, :]
@@ -185,8 +204,17 @@
             expo = jnp.exp2((scores - peak) * factor).astype(jnp.bfloat16)
             shrink = jnp.exp2((before - peak) * factor)
             top[h : h + 1, :] = peak
-            value = jnp.concatenate([values[h, :, at] * flag for at, flag in zip(starts, flags)], axis=1)
+            value = jnp.concatenate([values[0, h * head : (h + 1) * head, at] for at in starts], axis=1)
+            value = jnp.concatenate([value, one], axis=0)
             acc[h] = acc[h] * shrink + jnp.dot(value, expo, preferred_element_type=jnp.float32)
+
+    @pl.loop(0, count // PAIR)
+    def _(step):
+        visit(step * PAIR, PAIR)
+
+    @pl.when(count % PAIR == 1)
+    def _():
+        visit(count - 1, 1)
 
     for h in range(H):
         amount = acc[h, head : head + 1, :]
@@ -254,16 +282,32 @@
     users, own_cands, embed = candidates.shape
     cands = n * own_cands
     line = n // 2
-    whole, weights = pl.pallas_call(
+    own_rows = history.shape[1]
+    blocks = own_rows // BLOCK
+    first = (lax.axis_index("hist") * blocks).astype(jnp.int32)
+    ids = first + jnp.arange(blocks, dtype=jnp.int32)
+    flags = jnp.any(selected[:, :, None] == ids[None, None, :], axis=1)
+    flags = jnp.logical_and(flags, ids[None, :] * BLOCK < lengths[:, None]).astype(jnp.int32)
+    base = first.reshape(1)
+    whole, weights, keys, values = pl.pallas_call(
         functools.partial(gather_kernel, n, ranks),
         out_shape=[
             jax.ShapeDtypeStruct((users, cands, embed), jnp.bfloat16),
             jax.ShapeDtypeStruct((projections.shape[0], ranks * projections.shape[1], embed), jnp.bfloat16),
+            jax.ShapeDtypeStruct((users, own_rows, embed), jnp.bfloat16),
+            jax.ShapeDtypeStruct((users, embed, own_rows), jnp.bfloat16),
         ],
-        in_specs=[pl.BlockSpec(memory_space=pltpu.VMEM)] * 2,
-        out_specs=[pl.BlockSpec(memory_space=pltpu.VMEM)] * 2,
+        in_specs=[pl.BlockSpec(memory_space=pltpu.SMEM)]
+        + [pl.BlockSpec(memory_space=pltpu.VMEM)] * 2
+        + [pl.BlockSpec(memory_space=pl.ANY)],
+        out_specs=[pl.BlockSpec(memory_space=pltpu.VMEM)] * 2 + [pl.BlockSpec(memory_space=pl.ANY)] * 2,
         scratch_shapes=[
+            pltpu.VMEM((users, own_rows, embed), jnp.bfloat16),
+            pltpu.VMEM((users, own_rows, embed), jnp.bfloat16),
+            pltpu.VMEM((users, embed, own_rows), jnp.bfloat16),
             pltpu.SemaphoreType.DMA((users + 1,)),
+            pltpu.SemaphoreType.DMA((users,)),
+            pltpu.SemaphoreType.DMA((2, users)),
             pltpu.SemaphoreType.DMA((line - 1, users)),
             pltpu.SemaphoreType.DMA((line - 1, users)),
             pltpu.SemaphoreType.DMA((line, users)),
@@ -273,10 +317,8 @@
         ],
         compiler_params=pltpu.CompilerParams(collective_id=1, has_side_effects=True),
         name="gather",
-    )(candidates, projections)
-    own_rows = history.shape[1]
+    )(lengths, candidates, projections, history)
     wide = -(-users * own_cands // 128) * 128
-    base = (lax.axis_index("hist") * (own_rows // BLOCK)).astype(jnp.int32).reshape(1)
     parts, stats = pl.pallas_call(
         functools.partial(attend_kernel, own_cands),
         grid_spec=pltpu.PrefetchScalarGridSpec(
@@ -285,6 +327,7 @@
             in_specs=[
                 pl.BlockSpec((1, cands, embed), lambda u, *_: (u, 0, 0)),
                 pl.BlockSpec((1, own_rows, embed), lambda u, *_: (u, 0, 0)),
+                pl.BlockSpec((1, embed, own_rows), lambda u, *_: (u, 0, 0)),
                 pl.BlockSpec((4, embed, embed), lambda u, *_: (0, 0, 0)),
             ],
             out_specs=[
@@ -293,13 +336,11 @@
             ],
             scratch_shapes=[
                 pltpu.VMEM((H, embed, cands), jnp.bfloat16),
-                pltpu.VMEM((own_rows, embed), jnp.bfloat16),
-                pltpu.VMEM((H, embed // H + 16, own_rows), jnp.bfloat16),
                 pltpu.VMEM((H, embed // H + 16, cands), jnp.float32),
                 pltpu.VMEM((8, cands), jnp.float32),
                 pltpu.VMEM((users, embed, cands), jnp.bfloat16),
                 pltpu.VMEM((users, H, cands), jnp.float32),
-                pltpu.SMEM((selected.shape[1] + 8,), jnp.int32),
+                pltpu.SMEM((blocks + 8,), jnp.int32),
             ],
         ),
         out_shape=[
@@ -307,7 +348,7 @@
             jax.ShapeDtypeStruct((n, H, wide), jnp.float32),
         ],
         name="attend",
-    )(lengths, selected, base, whole, history, weights)
+    )(lengths, flags, base, whole, keys, values, weights)
     result = pl.pallas_call(
         functools.partial(combine_kernel, n),
         out_shape=jax.ShapeDtypeStruct((wide, embed), jnp.bfloat16),

time: 67.3 us -> 66.3 us (0.985); the launches traced: 66.1 us -> 66.3 us
  other arithmetic: 0 us -> 2.22 us
  Pallas kernels: 64.6 us -> 62.5 us
    pallas_call x1, Pallas kernels: 30.4 us -> 23.1 us  [body(): pl.pallas_call(functools.partial(attend_kernel, own_cands), grid_spec=plt...]
    pallas_call x1, Pallas kernels: 19.9 us -> 24.6 us  [body(): pl.pallas_call(functools.partial(combine_kernel, n), out_shape=jax.ShapeD...]
    convert_element_type x0 -> x1, other arithmetic: none -> 1.33 us  [body(): jnp.logical_and(flags, ids[None, :] * BLOCK < lengths[:, None])]
    reduce_or x0 -> x1, other arithmetic: none -> 0.89 us  [body(): flags = jnp.any(selected[:, :, None] == ids[None, None, :], axis=1)]
where the time goes in v3:
time: 66.3 us
  Pallas kernels  62.5 us (94%)
  other arithmetic  2.22 us (3%)
  local copies, waits for them, and re-layouts  1.47 us (2%)
    pallas_call x1, Pallas kernels, body(): pl.pallas_call(functools.partial(combine_kernel, n), out_shape=jax.ShapeD...  24.6 us
    pallas_call x1, Pallas kernels, body(): pl.pallas_call(functools.partial(attend_kernel, own_cands), grid_spec=plt...  23.1 us
    pallas_call x1, Pallas kernels, body(): pl.pallas_call(functools.partial(gather_kernel, n, ranks), out_shape=[jax...  14.8 us
    unnamed x1, local copies, waits for them, and re-layouts  1.47 us
    convert_element_type x1, other arithmetic, body(): jnp.logical_and(flags, ids[None, :] * BLOCK < lengths[:, None])  1.33 us

profile of v3, /device:TPU:12, one launch (start us, length us, event | category | flops | bytes accessed | tf_op | source)
XLA Modules:
  0.0 66.3 jit_solution(281186297011173042)
XLA Ops:
  0.0 0.9 %compare_reduce_fusion = pred[4,16]{1,0:T(4,128)(4,1)S(1)} fusion(s32[4,64]{1,0:T(4,128)} %param.9, s32[16]{0:T(128)S(1)} %get-tuple-element.17), kind=kLoop, calls=%fused_computation | loop fusion | flops 8128 | bytes 1152 | tf_op jit(solution)/shard_map/reduce_or | solution.py:289
  0.9 1.3 %and_convert_fusion.flags = s32[4,16]{1,0:T(4,128)} fusion(pred[4,16]{1,0:T(4,128)(4,1)S(1)} %compare_reduce_fusion, s32[16]{0:T(128)S(1)} %get-tuple-element.18, s32[4]{0:T(128)} %lengths.3), kind=kLoop, calls=%fused_computation.1 | loop fusion | flops 192 | bytes 400 | tf_op jit(solution)/shard_map/convert_element_type | solution.py:290
  2.2 14.8 %gather.1 = (bf16[4,512,128]{2,1,0:T(8,128)(2,1)}, bf16[4,128,128]{2,1,0:T(8,128)(2,1)}, bf16[4,2048,128]{2,1,0:T(8,128)(2,1)}, bf16[4,128,2048]{2,1,0:T(8,128)(2,1)}) custom-call(s32[4]{0:T(128)} %lengths.3, bf16[4,64,128]{2,1,0:T(8,128)(2,1)} %cand.1, bf16[4,32,128]{2,1,0:T(8,128)(2,1)} %proj.1, bf16[4,2048,128]{2,1,0:T(8,128)(2,1)} %hist.1), custom_call_target="tpu_custom_call" | custom-call | tf_op jit(solution)/shard_map/gather/pallas_call | solution.py:292
  17.0 23.1 %attend.1 = (bf16[8,128,256]{2,1,0:T(8,128)(2,1)}, f32[8,4,256]{2,1,0:T(4,128)}) custom-call(s32[4]{0:T(128)} %lengths.3, s32[4,16]{1,0:T(4,128)} %and_convert_fusion.flags, s32[1]{0:T(128)} %bitcast.base, bf16[4,512,128]{2,1,0:T(8,128)(2,1)} %get-tuple-element.11.cand, bf16[4,2048,128]{2,1,0:T(8,128)(2,1)} %get-tuple-element.12.keys, ...), custom_call_target="tpu_custom_call" | custom-call | tf_op jit(solution)/shard_map/attend/pallas_call | solution.py:322
  40.1 24.6 %combine.1 = bf16[256,128]{1,0:T(8,128)(2,1)} custom-call(bf16[8,128,256]{2,1,0:T(8,128)(2,1)} %get-tuple-element.15.parts, f32[8,4,256]{2,1,0:T(4,128)} %get-tuple-element.16.stats, bf16[4,128,128]{2,1,0:T(8,128)(2,1)} %get-tuple-element.14.weights.out_weight), custom_call_target="tpu_custom_call" | custom-call | tf_op jit(solution)/shard_map/combine/pallas_call | solution.py:352
  64.8 1.5 %copy.7 = bf16[4,64,128]{2,1,0:T(8,128)(2,1)} copy(bf16[4,64,128]{2,1,0:T(8,128)(2,1)} %bitcast.2) | data formatting | bytes 131072
  (1 shorter events, 0.0 us)
